TPU v7x, 32 devices: a whole 2x2x4 slice. The times are simulated.
32 devices in a mesh: dp: 2 (over x), ep: 16 (over y, z, core).
Axes of the slice: x: 2, y: 2, z: 4, core: 2. Of those that a mesh axis runs over, the one named last changes fastest.
Arguments:
- x: bfloat16 [2, 16, 256, 3584], P('dp', 'ep'), parts along dimension 0
- expert: int32 [2, 16, 256, 8], P('dp', 'ep'), parts along dimension 0
- slot: int32 [2, 16, 256, 8], P('dp', 'ep'), parts along dimension 0
- gate: float32 [2, 16, 256, 8], P('dp', 'ep'), parts along dimension 0
- w_gate: bfloat16 [48, 3584, 2048], P('ep')
- w_up: bfloat16 [48, 3584, 2048], P('ep')
- w_down: bfloat16 [48, 2048, 3584], P('ep')
- s_gate: bfloat16 [3584, 2048], replicated
- s_up: bfloat16 [3584, 2048], replicated
- s_down: bfloat16 [2048, 3584], replicated
Outputs:
- y: bfloat16 [2, 16, 256, 3584], P('dp', 'ep'), parts along dimension 0
There are 2 independent parts. A program takes and returns all parts, laid end to end along the dimension named above; an argument that names none is the same for every part.
All inputs are finite; a program needn't handle non-finite values.
Results may differ from a plain program's by a relative error of at most 0.009.
Values are sent between devices in bfloat16 or wider.
A program may use at most 2 GiB of HBM per device.

v0:
```python
import jax
import jax.numpy as jnp
from jax import lax
from jax.sharding import NamedSharding, PartitionSpec as P


def einsum(form, a, b):
    return jnp.einsum(form, a.astype(jnp.float32), b.astype(jnp.float32))


def for_all(x, s_gate, s_up, s_down):
    h = jax.nn.silu(einsum("...d,df->...f", x, s_gate)) * einsum("...d,df->...f", x, s_up)
    return einsum("...f,fd->...d", h.astype(jnp.bfloat16), s_down)


def solution(mesh):
    def placed(v, *spec):
        return lax.with_sharding_constraint(v, NamedSharding(mesh, P(*spec)))

    def step(x, expert, slot, gate, w_gate, w_up, w_down, s_gate, s_up, s_down):
        experts, (tokens, top) = w_gate.shape[0], expert.shape[2:]
        slots = 5 * tokens * top // (4 * experts)
        to_expert = jax.nn.one_hot(expert, experts, dtype=jnp.bfloat16)
        to_slot = jax.nn.one_hot(slot, slots, dtype=jnp.bfloat16)
        weighted = to_expert * gate[..., None].astype(jnp.bfloat16)
        dispatch = einsum("abtke,abtkc->abtec", to_expert, to_slot).astype(jnp.bfloat16)
        combine = einsum("abtke,abtkc->abtec", weighted, to_slot).astype(jnp.bfloat16)
        z = einsum("abtec,abtd->aebcd", dispatch, x).astype(jnp.bfloat16)
        z = placed(z, "dp", None, "ep", None, None)
        z = placed(z, "dp", "ep", None, None, None)
        h = jax.nn.silu(einsum("aebcd,edf->aebcf", z, w_gate))
        h = (h * einsum("aebcd,edf->aebcf", z, w_up)).astype(jnp.bfloat16)
        out = einsum("aebcf,efd->aebcd", h, w_down).astype(jnp.bfloat16)
        out = placed(out, "dp", "ep", None, None, None)
        out = placed(out, "dp", None, "ep", None, None)
        y = einsum("abtec,aebcd->abtd", combine, out)
        return (y + for_all(x, s_gate, s_up, s_down)).astype(jnp.bfloat16)

    return step
```

profile of v0, /device:TPU:9, one launch (start us, length us, event | category | flops | bytes accessed | tf_op | source)
XLA Modules:
  0.0 1045.4 jit_solution(1092509388480181081)
XLA Ops:
  0.0 0.0 copy-start
  0.0 1.0 copy.11
  1.0 0.0 copy-start.1
  1.0 0.8 copy.9
  1.8 0.0 copy-start.3
  1.8 3.2 convolution_convert_fusion.1
  5.0 0.0 copy-done
  5.0 10.3 convolution_convert_fusion
  15.3 0.0 copy-done.1
  15.3 0.0 copy-done.3
  15.4 426.6 %all-to-all.4 = bf16[1,16,3,1,53,3584]{5,4,2,3,0,1:T(8,128)(2,1)} all-to-all(bf16[1,16,3,1,53,3584]{5,4,2,3,0,1:T(8,128)(2,1)} %bitcast.121), channel_id=1, replica_groups=mesh['dp'=2,'ep'=16] {'ep'}, dimensions={1} | all-to-all | bytes 36470784 | tf_op jit(solution)/sharding_constraint;jit(solution)/sharding_constraint | solution.py:18
  442.0 47.7 %fusion.2 = f32[3,16,53,2048]{3,2,1,0:T(8,128)} fusion(bf16[3,3584,2048]{2,1,0:T(8,128)(2,1)} %param.5, bf16[1,16,3,1,53,3584]{5,4,2,3,0,1:T(8,128)(2,1)} %all-to-all.4), kind=kOutput, calls=%fused_computation.2 | convolution fusion | flops 37346082816 | bytes 83116032 | tf_op jit(solution)/aebcd,edf->aebcf/dot_general | solution.py:8
  489.6 47.7 %fusion.4 = f32[3,16,53,2048]{3,2,1,0:T(8,128)} fusion(bf16[3,3584,2048]{2,1,0:T(8,128)(2,1)} %param.4, bf16[1,16,3,1,53,3584]{5,4,2,3,0,1:T(8,128)(2,1)} %all-to-all.4), kind=kOutput, calls=%fused_computation.4 | convolution fusion | flops 37346082816 | bytes 83116032 | tf_op jit(solution)/aebcd,edf->aebcf/dot_general | solution.py:8
  537.4 56.2 %convert_bitcast_fusion = bf16[1,3,16,1,53,3584]{5,4,2,1,3,0:T(8,128)(2,1)} fusion(bf16[3,2048,3584]{2,1,0:T(8,128)(2,1)} %param.6, f32[3,16,53,2048]{3,2,1,0:T(8,128)} %fusion.2, f32[3,16,53,2048]{3,2,1,0:T(8,128)} %fusion.4), kind=kOutput, calls=%fused_computation.15 | convolution fusion | flops 37386461184 | bytes 103956480 | tf_op jit(solution)/aebcf,efd->aebcd/dot_general | solution.py:8
  593.5 15.6 %copy.15 = bf16[1,3,16,1,53,3584]{5,4,1,3,0,2:T(8,128)(2,1)} copy(bf16[1,3,16,1,53,3584]{5,4,2,1,3,0:T(8,128)(2,1)} %convert_bitcast_fusion) | data formatting | bytes 36470784 | tf_op jit(solution)/sharding_constraint;jit(solution)/sharding_constraint | solution.py:18
  609.1 0.0 copy-start.5
  609.1 0.0 copy-start.2
  609.1 0.0 copy-start.4
  609.1 6.9 all-to-all-start.1
  616.0 0.0 copy-done.5
  616.0 0.1 copy.10
  616.1 0.0 copy-done.2
  616.1 0.0 copy-done.4
  616.2 4.3 convolution_convert_fusion.2
  620.5 8.8 convolution_bitcast_fusion.2
  629.3 19.8 %fusion.36 = f32[256,3584]{1,0:T(8,128)} fusion(bf16[2048,3584]{1,0:T(8,128)(2,1)} %param.9, bf16[3584,2048]{1,0:T(8,128)(2,1)} %param.8, f32[1,1,256,2048]{3,2,1,0:T(8,128)} %convolution_bitcast_fusion.2, bf16[1,1,256,3584]{3,2,1,0:T(8,128)(2,1)S(1)} %copy-done), kind=kOutput, calls=%fused_computation.41 | convolution fusion | flops 7519338496 | bytes 36962304 | tf_op jit(solution)/...f,fd->...d/dot_general | solution.py:8
  649.0 382.8 %all-to-all-done.1 = bf16[1,3,16,1,53,3584]{5,4,1,3,0,2:T(8,128)(2,1)} async-done(((bf16[1,3,16,1,53,3584]{5,4,1,3,0,2:T(8,128)(2,1)}), bf16[1,3,16,1,53,3584]{5,4,1,3,0,2:T(8,128)(2,1)}, u32[]{:S(2)}, u32[]{:S(2)}) %all-to-all-start.1) | async-done | bytes 18235424 | tf_op jit(solution)/sharding_constraint;jit(solution)/sharding_constraint | solution.py:18
  1031.8 13.6 %fusion.20 = bf16[1,1,256,3584]{3,2,1,0:T(8,128)(2,1)} fusion(f32[256,3584]{1,0:T(8,128)} %fusion.36, bf16[48,53,3584]{2,1,0:T(8,128)(2,1)} %bitcast.24, bf16[256,48,53]{2,1,0:T(8,128)(2,1)} %convolution_convert_fusion.2), kind=kOutput, calls=%fused_computation.23 | convolution fusion | flops 4670095360 | bytes 25042944 | tf_op jit(solution)/abtec,aebcd->abtd/dot_general | solution.py:8
  (1 shorter events, 0.0 us)
Async XLA Ops:
  0.0 5.0 copy-start
  1.0 14.4 %copy-start.1 = (s32[256,8]{1,0:T(8,128)}, s32[256,8]{1,0:T(8,128)S(1)}, u32[]{:S(2)}) copy-start(s32[256,8]{1,0:T(8,128)S(1)} %copy.11) | copy-start | bytes 24580
  1.8 13.5 %copy-start.3 = (s32[256,8]{1,0:T(8,128)}, s32[256,8]{1,0:T(8,128)S(1)}, u32[]{:S(2)}) copy-start(s32[256,8]{1,0:T(8,128)S(1)} %copy.9) | copy-start | bytes 24580
  609.1 6.9 copy-start.5
  609.1 7.1 copy-start.2
  609.1 7.1 copy-start.4
  609.1 422.7 %all-to-all-start.1 = ((bf16[1,3,16,1,53,3584]{5,4,1,3,0,2:T(8,128)(2,1)}), bf16[1,3,16,1,53,3584]{5,4,1,3,0,2:T(8,128)(2,1)}, u32[]{:S(2)}, u32[]{:S(2)}) async-start(bf16[1,3,16,1,53,3584]{5,4,1,3,0,2:T(8,128)(2,1)} %copy.15), calls=%async_computation.1 | async-start | bytes 38535168 | tf_op jit(solution)/sharding_constraint;jit(solution)/sharding_constraint | solution.py:18
where the time goes:
time: 1050 us
  blocking collectives  427 us (41%)
  waiting for transfers between devices  383 us (36%)
  matrix products  212 us (20%)
  local copies, waits for them, and re-layouts  17.5 us (2%)
    another operation x1, blocking collectives, placed(): return lax.with_sharding_constraint(v, NamedSharding(mesh, P(*spec)))  427 us
    another operation x1, waiting for transfers between devices, placed(): return lax.with_sharding_constraint(v, NamedSharding(mesh, P(*spec)))  383 us
    dot_general x9, matrix products, einsum(): return jnp.einsum(form, a.astype(jnp.float32), b.astype(jnp.float32))  212 us
  transfers between devices with their start and end apart: 1, of which 1 were waited for; matrix products, arithmetic and copies ran while one was open for 3% of the time, Pallas kernels for 0%

commit v1 on v0

v1 whole, which is shorter than its diff:
```python
import jax
import jax.numpy as jnp
from jax import lax
from jax.sharding import PartitionSpec as P


def mm(form, a, b):
    return jnp.einsum(form, a, b, preferred_element_type=jnp.float32)


def solution(mesh):
    def step(x, expert, slot, gate, w_gate, w_up, w_down, s_gate, s_up, s_down):
        members = mesh.shape["ep"]
        experts, (tokens, top) = w_gate.shape[0], expert.shape[2:]
        slots = 5 * tokens * top // (4 * experts)
        own = experts // members
        pad = -(-slots // 8) * 8

        def device(x, expert, slot, gate, w_gate, w_up, w_down, s_gate, s_up, s_down):
            x, expert, slot, gate = x[0, 0], expert[0, 0], slot[0, 0], gate[0, 0]
            me = lax.axis_index("ep")
            code = jnp.where(slot < slots, expert * pad + slot, -1).astype(jnp.float32)
            info = jnp.concatenate([code, gate.astype(jnp.bfloat16).astype(jnp.float32)], axis=1)
            info = lax.all_gather(info, "ep")
            xs = lax.all_gather(x, "ep")
            row = info[..., :top].astype(jnp.int32) - me * own * pad
            weight = info[..., top:]
            rows = own * pad
            take = jnp.zeros((members, rows, tokens), jnp.float32)
            give = jnp.zeros((members, tokens, rows), jnp.float32)
            for j in range(top):
                r = row[..., j]
                take += (r[:, None, :] == jnp.arange(rows)[None, :, None]).astype(jnp.float32)
                give += jnp.where(r[..., None] == jnp.arange(rows), weight[..., j, None], 0.0)
            take, give = take.astype(jnp.bfloat16), give.astype(jnp.bfloat16)
            z = mm("srt,std->srd", take, xs).astype(jnp.bfloat16)
            z = z.reshape(members, own, pad, -1).transpose(1, 0, 2, 3).reshape(own, members * pad, -1)
            h = jax.nn.silu(mm("erd,edf->erf", z, w_gate)) * mm("erd,edf->erf", z, w_up)
            out = mm("erf,efd->erd", h.astype(jnp.bfloat16), w_down).astype(jnp.bfloat16)
            out = out.reshape(own, members, pad, -1).transpose(1, 0, 2, 3).reshape(members, rows, -1)
            part = mm("str,srd->std", give, out).astype(jnp.bfloat16)
            y = lax.psum_scatter(part, "ep", scatter_dimension=0)
            hs = jax.nn.silu(mm("td,df->tf", x, s_gate)) * mm("td,df->tf", x, s_up)
            shared = mm("tf,fd->td", hs.astype(jnp.bfloat16), s_down)
            return (y.astype(jnp.float32) + shared).astype(jnp.bfloat16)[None, None]

        tok, exp, rep = P("dp", "ep"), P("ep"), P()
        return jax.shard_map(
            device, mesh=mesh,
            in_specs=(tok, tok, tok, tok, exp, exp, exp, rep, rep, rep),
            out_specs=tok, check_vma=False,
        )(x, expert, slot, gate, w_gate, w_up, w_down, s_gate, s_up, s_down)

    return step
```

time: 1050 us -> 690 us (0.66)
  the two profiles are of different devices: /device:TPU:9 before, /device:TPU:0 now
where the time goes in v1:
time: 690 us
  waiting for transfers between devices  380 us (55%)
  matrix products  235 us (34%)
  local copies, waits for them, and re-layouts  33.4 us (5%)
  blocking collectives  25.8 us (4%)
  between operations  13.8 us (2%)
    reduce_scatter x1, waiting for transfers between devices, device(): y = lax.psum_scatter(part, 'ep', scatter_dimension=0)  253 us
    dot_general x8, matrix products, mm(): return jnp.einsum(form, a, b, preferred_element_type=jnp.float32)  235 us
    all_gather x1, waiting for transfers between devices, device(): xs = lax.all_gather(x, 'ep')  126 us
    all_gather x1, blocking collectives, device(): info = lax.all_gather(info, 'ep')  25.8 us
    transpose x1, local copies, waits for them, and re-layouts, device(): z.reshape(members, own, pad, -1).transpose(1, 0, 2, 3)  15.6 us
    transpose x1, local copies, waits for them, and re-layouts, device(): out.reshape(own, members, pad, -1).transpose(1, 0, 2, 3)  15.5 us
  transfers between devices with their start and end apart: 2, of which 2 were waited for; matrix products, arithmetic and copies ran while one was open for 3% of the time, Pallas kernels for 0%

profile of v1, /device:TPU:0, one launch (start us, length us, event | category | flops | bytes accessed | tf_op | source)
XLA Modules:
  0.0 689.7 jit_solution(14112229366930177023)
XLA Ops:
  6.5 0.0 all-gather.4.cloned.1.call-start
  6.5 0.7 all-gather.4.cloned.1.call-update
  7.3 0.0 reduce-scatter.2.cloned.1.call-start
  7.3 0.7 bitcast_convert_fusion
  8.0 0.7 convert_bitcast_fusion
  8.7 25.8 %all-gather = f32[4096,16]{0,1:T(8,128)S(1)} all-gather(f32[256,16]{0,1:T(8,128)S(1)} %pad_maximum_fusion), channel_id=2, replica_groups=mesh['dp'=2,'ep'=16] {'ep'}, dimensions={0}, use_global_device_ids=true | all-gather | bytes 278528 | tf_op jit(solution)/shard_map/all_gather | solution.py:24
  34.5 0.1 copy.16
  34.6 0.6 slice_bitcast_fusion.14
  35.3 0.0 copy-start.1
  35.3 0.0 copy-start.3
  35.3 0.0 copy-start.5
  35.3 0.0 copy-start.7
  35.3 0.0 copy-start.9
  35.3 0.0 copy-start.11
  35.4 0.0 copy-start.13
  35.4 0.0 copy-start.15
  35.4 126.1 %all-gather.4.cloned.1.call-done = bf16[16,1,256,3584]{3,2,1,0:T(8,128)(2,1)} async-done(((bf16[1,1,256,3584]{3,2,1,0:T(8,128)(2,1)}), bf16[16,1,256,3584]{3,2,1,0:T(8,128)(2,1)}) %all-gather.4.cloned.1.call-update) | async-done | bytes 29360144 | tf_op jit(solution)/shard_map/all_gather | solution.py:25
  161.5 28.0 %fusion.2 = bf16[16,168,3584]{2,1,0:T(8,128)(2,1)} fusion(bf16[16,1,256,3584]{3,2,1,0:T(8,128)(2,1)} %all-gather.4.cloned.1.call-done, s32[16,256]{1,0:T(8,128)S(1)} %get-tuple-element.14, s32[16,256]{1,0:T(8,128)S(1)} %get-tuple-element.15, s32[16,256]{1,0:T(8,128)S(1)} %get-tuple-element.16, s32[16,256]{1,0:T(8,128)S(1)} %get-tuple-element.17, ...), kind=kOutput, calls=%fused_computation.4 | convolution fusion | flops 4958650368 | bytes 48758784 | tf_op jit(solution)/shard_map/srt,std->srd/dot_general | solution.py:8
  189.5 0.0 copy-done.1
  189.5 0.0 copy-done.3
  189.5 0.0 copy-done.5
  189.5 0.0 copy-done.7
  189.5 0.0 copy-done.9
  189.5 0.0 copy-done.11
  189.5 0.0 copy-done.13
  189.5 0.0 copy-done.15
  189.5 15.6 %copy.14 = bf16[3,16,56,3584]{3,2,1,0:T(8,128)(2,1)} copy(bf16[3,16,56,3584]{3,2,0,1:T(8,128)(2,1)} %bitcast.75) | data formatting | bytes 38535168 | tf_op jit(solution)/shard_map/transpose | solution.py:37
  205.1 50.2 %fusion.40 = f32[3,896,2048]{2,1,0:T(8,128)} fusion(bf16[3,896,3584]{2,1,0:T(8,128)(2,1)} %bitcast.77, bf16[3,3584,2048]{2,1,0:T(8,128)(2,1)} %param.14), kind=kOutput, calls=%fused_computation.81 | convolution fusion | flops 39460012032 | bytes 85327872 | tf_op jit(solution)/shard_map/erd,edf->erf/dot_general | solution.py:8
  255.3 50.2 %fusion.41 = f32[3,896,2048]{2,1,0:T(8,128)} fusion(bf16[3,896,3584]{2,1,0:T(8,128)(2,1)} %bitcast.78, bf16[3,3584,2048]{2,1,0:T(8,128)(2,1)} %param.15), kind=kOutput, calls=%fused_computation.82 | convolution fusion | flops 39460012032 | bytes 85327872 | tf_op jit(solution)/shard_map/erd,edf->erf/dot_general | solution.py:8
  305.4 57.0 %convolution_convert_fusion.1 = bf16[3,896,3584]{2,1,0:T(8,128)(2,1)} fusion(bf16[3,2048,3584]{2,1,0:T(8,128)(2,1)} %param.16, f32[3,896,2048]{2,1,0:T(8,128)} %fusion.41, f32[3,896,2048]{2,1,0:T(8,128)} %fusion.40), kind=kOutput, calls=%fused_computation.5 | convolution fusion | flops 39502675968 | bytes 107347968 | tf_op jit(solution)/shard_map/erf,efd->erd/dot_general | solution.py:8
  362.4 0.0 copy-start.8
  362.4 0.0 copy-start.10
  362.4 0.0 copy-start.12
  362.4 0.0 copy-start.14
  362.4 0.0 copy-start.16
  362.4 0.0 copy-start.17
  362.5 0.0 copy-start.18
  362.5 0.0 copy-start.19
  362.5 0.0 copy-start.20
  362.5 0.0 copy-start.21
  362.5 0.0 copy-start.22
  362.5 0.0 copy-start.23
  362.5 0.0 copy-start.24
  362.5 15.5 %copy.15 = bf16[16,3,56,3584]{3,2,1,0:T(8,128)(2,1)} copy(bf16[16,3,56,3584]{3,2,0,1:T(8,128)(2,1)} %bitcast.79) | data formatting | bytes 38535168 | tf_op jit(solution)/shard_map/transpose | solution.py:40
  378.1 0.0 copy-done.2
  378.1 0.0 copy-done.4
  378.1 0.0 copy-done.6
  378.1 0.0 copy-done.8
  378.1 0.0 copy-done.10
  378.1 0.0 copy-done.12
  378.1 0.0 copy-done.14
  378.1 0.0 copy-done.16
  378.1 0.0 copy-done.17
  378.1 0.0 copy-done.18
  378.1 0.0 copy-done.19
  378.1 0.0 copy-done.20
  378.2 0.0 copy-done.21
  378.2 22.5 %convolution_convert_fusion = bf16[16,256,3584]{2,1,0:T(8,128)(2,1)} fusion(bf16[16,168,3584]{2,1,0:T(8,128)(2,1)} %bitcast.76, f32[16,256]{1,0:T(8,128)S(1)} %copy-done.18, s32[16,256]{1,0:T(8,128)S(1)} %copy-done.4, f32[16,256]{1,0:T(8,128)S(1)} %copy-done.19, s32[16,256]{1,0:T(8,128)S(1)} %copy-done.6, f32[16,256]{1,0:T(8,128)S(1)} %copy-done.20, ...), kind=kOutput, calls=%fused_computation.2 | convolution fusion | flops 4963696640 | bytes 48889856 | tf_op jit(solution)/shard_map/str,srd->std/dot_general | solution.py:8
  400.7 0.0 reduce-scatter.2.cloned.1.call-update
  400.7 1.5 copy-done
  402.2 7.5 %fusion.10 = f32[256,2048]{1,0:T(8,128)S(1)} fusion(bf16[3584,2048]{1,0:T(8,128)(2,1)} %param.17, bf16[1,1,256,3584]{3,2,1,0:T(8,128)(2,1)S(1)} %copy-done), kind=kOutput, calls=%fused_computation.31 | convolution fusion | flops 3758096384 | bytes 18612224 | tf_op jit(solution)/shard_map/td,df->tf/dot_general | solution.py:8
  409.7 9.4 %fusion.8 = bf16[256,2048]{1,0:T(8,128)(2,1)S(1)} fusion(bf16[3584,2048]{1,0:T(8,128)(2,1)} %param.18, f32[256,2048]{1,0:T(8,128)S(1)} %fusion.10, bf16[1,1,256,3584]{3,2,1,0:T(8,128)(2,1)S(1)} %copy-done), kind=kOutput, calls=%fused_computation.29 | convolution fusion | flops 3761242112 | bytes 19660800 | tf_op jit(solution)/shard_map/td,df->tf/dot_general | solution.py:8
  419.2 253.1 %reduce-scatter.2.cloned.1.call-done = bf16[1,256,3584]{2,1,0:T(8,128)(2,1)} async-done(((bf16[16,256,3584]{2,1,0:T(8,128)(2,1)}), bf16[1,256,3584]{2,1,0:T(8,128)(2,1)}) %reduce-scatter.2.cloned.1.call-update) | async-done | bytes 1835024 | tf_op jit(solution)/shard_map/reduce_scatter | solution.py:42
  672.2 10.6 %fusion.7 = bf16[1,1,256,3584]{3,2,1,0:T(8,128)(2,1)} fusion(bf16[256,2048]{1,0:T(8,128)(2,1)S(1)} %fusion.8, bf16[2048,3584]{1,0:T(8,128)(2,1)} %param.19, bf16[1,256,3584]{2,1,0:T(8,128)(2,1)} %reduce-scatter.2.cloned.1.call-done), kind=kOutput, calls=%fused_computation.9 | convolution fusion | flops 3760848896 | bytes 19398656 | tf_op jit(solution)/shard_map/tf,fd->td/dot_general | solution.py:8
  (10 shorter events, 0.0 us)
Async XLA Ops:
  6.5 154.9 %all-gather.4.cloned.1.call-start = ((), (), s32[]{:S(2)}) async-start(), calls=%async_computation.2 | async-start | bytes 31195136 | tf_op jit(solution)/shard_map/all_gather | solution.py:25
  7.3 665.0 %reduce-scatter.2.cloned.1.call-start = ((), (), s32[]{:S(2)}) async-start(), calls=%async_computation.1 | async-start | bytes 31195136 | tf_op jit(solution)/shard_map/reduce_scatter | solution.py:42
  35.3 154.2 %copy-start.1 = (s32[16,256]{1,0:T(8,128)}, s32[16,256]{1,0:T(8,128)S(1)}, u32[]{:S(2)}) copy-start(s32[16,256]{1,0:T(8,128)S(1)} %get-tuple-element.13) | copy-start | bytes 49156
  35.3 154.2 %copy-start.3 = (s32[16,256]{1,0:T(8,128)}, s32[16,256]{1,0:T(8,128)S(1)}, u32[]{:S(2)}) copy-start(s32[16,256]{1,0:T(8,128)S(1)} %get-tuple-element.14) | copy-start | bytes 49156
  35.3 154.1 %copy-start.5 = (s32[16,256]{1,0:T(8,128)}, s32[16,256]{1,0:T(8,128)S(1)}, u32[]{:S(2)}) copy-start(s32[16,256]{1,0:T(8,128)S(1)} %get-tuple-element.15) | copy-start | bytes 49156
  35.3 154.1 %copy-start.7 = (s32[16,256]{1,0:T(8,128)}, s32[16,256]{1,0:T(8,128)S(1)}, u32[]{:S(2)}) copy-start(s32[16,256]{1,0:T(8,128)S(1)} %get-tuple-element.16) | copy-start | bytes 49156
  35.3 154.1 %copy-start.9 = (s32[16,256]{1,0:T(8,128)}, s32[16,256]{1,0:T(8,128)S(1)}, u32[]{:S(2)}) copy-start(s32[16,256]{1,0:T(8,128)S(1)} %get-tuple-element.17) | copy-start | bytes 49156
  35.3 154.1 %copy-start.11 = (s32[16,256]{1,0:T(8,128)}, s32[16,256]{1,0:T(8,128)S(1)}, u32[]{:S(2)}) copy-start(s32[16,256]{1,0:T(8,128)S(1)} %get-tuple-element.18) | copy-start | bytes 49156
  35.4 154.1 %copy-start.13 = (s32[16,256]{1,0:T(8,128)}, s32[16,256]{1,0:T(8,128)S(1)}, u32[]{:S(2)}) copy-start(s32[16,256]{1,0:T(8,128)S(1)} %get-tuple-element.19) | copy-start | bytes 49156
  35.4 154.1 %copy-start.15 = (s32[16,256]{1,0:T(8,128)}, s32[16,256]{1,0:T(8,128)S(1)}, u32[]{:S(2)}) copy-start(s32[16,256]{1,0:T(8,128)S(1)} %get-tuple-element.20) | copy-start | bytes 49156
  362.4 15.7 %copy-start.2 = (s32[16,256]{1,0:T(8,128)S(1)}, s32[16,256]{1,0:T(8,128)}, u32[]{:S(2)}) copy-start(s32[16,256]{1,0:T(8,128)} %copy-done.1) | copy-start | bytes 49156
  362.4 15.7 %copy-start.4 = (s32[16,256]{1,0:T(8,128)S(1)}, s32[16,256]{1,0:T(8,128)}, u32[]{:S(2)}) copy-start(s32[16,256]{1,0:T(8,128)} %copy-done.3) | copy-start | bytes 49156
  362.4 15.7 %copy-start.6 = (s32[16,256]{1,0:T(8,128)S(1)}, s32[16,256]{1,0:T(8,128)}, u32[]{:S(2)}) copy-start(s32[16,256]{1,0:T(8,128)} %copy-done.5) | copy-start | bytes 49156
  362.4 15.7 %copy-start.8 = (s32[16,256]{1,0:T(8,128)S(1)}, s32[16,256]{1,0:T(8,128)}, u32[]{:S(2)}) copy-start(s32[16,256]{1,0:T(8,128)} %copy-done.7) | copy-start | bytes 49156
  362.4 15.7 %copy-start.10 = (s32[16,256]{1,0:T(8,128)S(1)}, s32[16,256]{1,0:T(8,128)}, u32[]{:S(2)}) copy-start(s32[16,256]{1,0:T(8,128)} %copy-done.9) | copy-start | bytes 49156
  362.4 15.7 %copy-start.12 = (s32[16,256]{1,0:T(8,128)S(1)}, s32[16,256]{1,0:T(8,128)}, u32[]{:S(2)}) copy-start(s32[16,256]{1,0:T(8,128)} %copy-done.11) | copy-start | bytes 49156
  362.4 15.7 %copy-start.14 = (s32[16,256]{1,0:T(8,128)S(1)}, s32[16,256]{1,0:T(8,128)}, u32[]{:S(2)}) copy-start(s32[16,256]{1,0:T(8,128)} %copy-done.13) | copy-start | bytes 49156
  362.4 15.7 %copy-start.16 = (s32[16,256]{1,0:T(8,128)S(1)}, s32[16,256]{1,0:T(8,128)}, u32[]{:S(2)}) copy-start(s32[16,256]{1,0:T(8,128)} %copy-done.15) | copy-start | bytes 49156
  362.4 15.7 %copy-start.17 = (f32[16,256]{1,0:T(8,128)S(1)}, f32[16,256]{1,0:T(8,128)}, u32[]{:S(2)}) copy-start(f32[16,256]{1,0:T(8,128)} %get-tuple-element.5) | copy-start | bytes 49156
  362.5 15.7 %copy-start.18 = (f32[16,256]{1,0:T(8,128)S(1)}, f32[16,256]{1,0:T(8,128)}, u32[]{:S(2)}) copy-start(f32[16,256]{1,0:T(8,128)} %get-tuple-element.6) | copy-start | bytes 49156
  362.5 15.7 %copy-start.19 = (f32[16,256]{1,0:T(8,128)S(1)}, f32[16,256]{1,0:T(8,128)}, u32[]{:S(2)}) copy-start(f32[16,256]{1,0:T(8,128)} %get-tuple-element.7) | copy-start | bytes 49156
  362.5 15.7 %copy-start.20 = (f32[16,256]{1,0:T(8,128)S(1)}, f32[16,256]{1,0:T(8,128)}, u32[]{:S(2)}) copy-start(f32[16,256]{1,0:T(8,128)} %get-tuple-element.8) | copy-start | bytes 49156
  362.5 15.7 %copy-start.21 = (f32[16,256]{1,0:T(8,128)S(1)}, f32[16,256]{1,0:T(8,128)}, u32[]{:S(2)}) copy-start(f32[16,256]{1,0:T(8,128)} %get-tuple-element.9) | copy-start | bytes 49156
  362.5 15.7 %copy-start.22 = (f32[16,256]{1,0:T(8,128)S(1)}, f32[16,256]{1,0:T(8,128)}, u32[]{:S(2)}) copy-start(f32[16,256]{1,0:T(8,128)} %get-tuple-element.10) | copy-start | bytes 49156
  362.5 15.7 %copy-start.23 = (f32[16,256]{1,0:T(8,128)S(1)}, f32[16,256]{1,0:T(8,128)}, u32[]{:S(2)}) copy-start(f32[16,256]{1,0:T(8,128)} %get-tuple-element.11) | copy-start | bytes 49156
  362.5 15.7 %copy-start.24 = (f32[16,256]{1,0:T(8,128)S(1)}, f32[16,256]{1,0:T(8,128)}, u32[]{:S(2)}) copy-start(f32[16,256]{1,0:T(8,128)} %get-tuple-element.12) | copy-start | bytes 49156
  400.7 1.5 copy-start
Sparse Core Ops, SparseCore 0:
  8.9 152.5 all-gather.3
  400.8 271.3 reduce-scatter.1

commit v2 on v1

v2 whole, which is shorter than its diff:
```python
import functools

import jax
import jax.numpy as jnp
from jax import lax
from jax.experimental import pallas as pl
from jax.experimental.pallas import tpu as pltpu
from jax.sharding import PartitionSpec as P

MESH = pl.DeviceIdType.MESH
F32, BF16 = jnp.float32, jnp.bfloat16
CHIPS = 8
HALF = 256
UNIT = 2 * HALF
TILE = 256


def dot(a, b):
    return jnp.dot(a, b, preferred_element_type=F32)


def chip_at(pos):
    return pos + pos // 4 * (11 - 2 * pos)


def places():
    me = lax.axis_index("ep")
    core, pos = me % 2, chip_at(me // 2)

    def device(pos, core):
        return (lax.axis_index("dp"), 2 * chip_at(pos) + core)

    right, left = device((pos + 1) % CHIPS, core), device((pos + CHIPS - 1) % CHIPS, core)
    return core, pos, right, left, device(pos, 1 - core)


def meet(devices):
    barrier = pltpu.get_barrier_semaphore()
    for d in devices:
        pl.semaphore_signal(barrier, inc=1, device_id=d, device_id_type=MESH)
    pl.semaphore_wait(barrier, len(devices))


def gather_up(
    x_ref, take_ref, wg_ref, wu_ref, sg_ref, su_ref, all_ref, h_ref, hs_ref,
    acc, acc_s, xbuf, z, wbuf, hbuf,
    send_sem, recv_sem, psend_sem, precv_sem, load_sem, w_sem, h_sem,
):
    own, total, ff = acc.shape[1:]
    tokens, d = x_ref.shape
    units = d // UNIT
    sources = 2 * CHIPS
    pad = total // sources
    core, pos, right, left, partner = places()
    ahead = (right, left)
    meet((right, left, partner))

    def origin(way, hop):
        return (pos - hop + CHIPS) % CHIPS if way == 0 else (pos + hop) % CHIPS

    def cols(j, way):
        return pl.ds(pl.multiple_of(j * UNIT + way * HALF, HALF), HALF)

    def ring(j, way, hop):
        here = all_ref.at[core, origin(way, hop), :, cols(j, way)]
        src = x_ref.at[:, cols(j, way)] if hop == 0 else here
        return pltpu.make_async_remote_copy(
            src_ref=src, dst_ref=here, send_sem=send_sem.at[way, j, hop],
            recv_sem=recv_sem.at[way, j, hop], device_id=ahead[way], device_id_type=MESH)

    def arrival(j, way, hop):
        there = all_ref.at[core, origin(way, hop), :, cols(j, way)]
        return pltpu.make_async_remote_copy(
            src_ref=there, dst_ref=there, send_sem=send_sem.at[way, j, hop - 1],
            recv_sem=recv_sem.at[way, j, hop - 1], device_id=ahead[way], device_id_type=MESH)

    def pair(j, way, hop):
        here = all_ref.at[core, origin(way, hop), :, cols(j, way)]
        src = x_ref.at[:, cols(j, way)] if hop == 0 else here
        return pltpu.make_async_remote_copy(
            src_ref=src, dst_ref=here, send_sem=psend_sem.at[way, j, hop],
            recv_sem=precv_sem.at[way, j, hop], device_id=partner, device_id_type=MESH)

    def pair_arrival(j, way, hop):
        there = all_ref.at[1 - core, origin(way, hop), :, cols(j, way)]
        return pltpu.make_async_remote_copy(
            src_ref=there, dst_ref=there, send_sem=psend_sem.at[way, j, hop],
            recv_sem=precv_sem.at[way, j, hop], device_id=partner, device_id_type=MESH)

    def load(j, color, place):
        wide = pl.ds(pl.multiple_of(j * UNIT, UNIT), UNIT)
        s = color * CHIPS + place
        return pltpu.make_async_copy(all_ref.at[color, place, :, wide], xbuf.at[s], load_sem.at[s])

    def load_own(j):
        wide = pl.ds(pl.multiple_of(j * UNIT, UNIT), UNIT)
        s = core * CHIPS + pos
        return pltpu.make_async_copy(x_ref.at[:, wide], xbuf.at[s], load_sem.at[s])

    mats = [sg_ref, su_ref] + [m.at[e] for e in range(own) for m in (wg_ref, wu_ref)]
    count = len(mats)

    def weight(j, k):
        rows = pl.ds(pl.multiple_of(j * UNIT, UNIT), UNIT)
        return pltpu.make_async_copy(mats[k].at[rows, :], wbuf.at[k % 2], w_sem.at[k % 2])

    def send(j, hop):
        for way in range(2):
            if hop > 0:
                arrival(j, way, hop).wait_recv()
            if hop < CHIPS - 1:
                ring(j, way, hop).start()
            pair(j, way, hop).start()

    def product(j, k):
        weight(j, k).wait()
        if k + 1 < count:
            weight(j, k + 1).start()
        else:
            @pl.when(j + 1 < units)
            def _():
                weight(j + 1, 0).start()
        w = wbuf.at[k % 2]
        e, up = (k - 2) // 2, k % 2
        if k < 2:
            lhs, total_ref = xbuf.at[core * CHIPS + pos], acc_s.at[up]
        else:
            lhs, total_ref = z.at[e], acc.at[up, e]

        @pl.loop(0, ff // TILE)
        def _(n):
            at = pl.ds(pl.multiple_of(n * TILE, TILE), TILE)
            total_ref[:, at] += dot(lhs[...], w[:, at])

    def finish(e):
        gate = acc_s.at[0] if e == own else acc.at[0, e]
        up = acc_s.at[1] if e == own else acc.at[1, e]
        n_rows = tokens if e == own else total
        out = hs_ref if e == own else h_ref.at[e]

        def put(n, b):
            at = pl.ds(pl.multiple_of(n * TILE, TILE), TILE)
            return pltpu.make_async_copy(hbuf.at[b, pl.ds(0, n_rows)], out.at[:, at], h_sem.at[b])

        @pl.loop(0, ff // TILE, step=2)
        def _(n):
            for b in range(2):
                at = pl.ds(pl.multiple_of((n + b) * TILE, TILE), TILE)

                @pl.when(n > 0)
                def _():
                    put(n + b - 2, b).wait()
                g = gate[:, at]
                hbuf[b, pl.ds(0, n_rows)] = (g * jax.nn.sigmoid(g) * up[:, at]).astype(BF16)
                put(n + b, b).start()
        for b in range(2):
            put(ff // TILE - 2 + b, b).wait()

    weight(0, 0).start()

    @pl.loop(0, ff // TILE)
    def _(n):
        at = pl.ds(pl.multiple_of(n * TILE, TILE), TILE)
        for g in range(2):
            acc_s[g, :, at] = jnp.zeros((tokens, TILE), F32)
            for e in range(own):
                acc[g, e, :, at] = jnp.zeros((total, TILE), F32)

    @pl.loop(0, units + 3)
    def _(u):
        for i in range(7):
            back, hop = (0, i // 2) if i % 2 == 0 else (1, i // 2 + 4)

            @pl.when(jnp.logical_and(u - back >= 0, u - back < units))
            def _():
                send(u - back, hop)
            now = u - 2
            if i == 0:
                @pl.when(jnp.logical_and(now >= 0, now < units))
                def _():
                    send(now, CHIPS - 1)
                    load_own(now).start()
                    for hop in range(1, CHIPS):
                        load(now, core, origin(0, hop)).start()
                    for hop in range(CHIPS - 1):
                        for way in range(2):
                            pair_arrival(now, way, hop).wait_recv()
                    for hop in (0, 2, 3, 4, 5, 6):
                        load(now, 1 - core, origin(0, hop)).start()

                @pl.when(jnp.logical_and(now - 1 >= 0, now - 1 < units))
                def _():
                    product(now - 1, count - 1)
            else:
                @pl.when(jnp.logical_and(now >= 0, now < units))
                def _():
                    if i == 1:
                        for way in range(2):
                            pair_arrival(now, way, CHIPS - 1).wait_recv()
                        for hop in (1, CHIPS - 1):
                            load(now, 1 - core, origin(0, hop)).start()
                        load_own(now).wait()
                        for hop in range(1, CHIPS):
                            load(now, core, origin(0, hop)).wait()
                        for hop in range(CHIPS):
                            load(now, 1 - core, origin(0, hop)).wait()
                        for s in range(sources):
                            rows = dot(take_ref[s], xbuf[s]).astype(BF16)
                            for e in range(own):
                                z[e, pl.ds(s * pad, pad), :] = rows[e * pad:(e + 1) * pad]
                        product(now, 0)
                        product(now, 1)
                    else:
                        product(now, i)

    for e in (own, *range(own)):
        finish(e)

    @pl.loop(0, units)
    def _(j):
        for way in range(2):
            for hop in range(CHIPS - 1):
                ring(j, way, hop).wait_send()
            for hop in range(CHIPS):
                pair(j, way, hop).wait_send()


def down_scatter(
    h_ref, hs_ref, give_ref, wd_ref, sd_ref, y_ref,
    part, shared, psend, precv, outs, wbuf, rbuf,
    send_sem, recv_sem, psend_sem, precv_sem, w_sem,
):
    own, total, ff = h_ref.shape
    tokens, d = y_ref.shape
    units = d // UNIT
    sources = 2 * CHIPS
    pad = total // sources
    core, pos, right, left, partner = places()
    ahead = (right, left)
    meet((right, left, partner))

    mats = [sd_ref] + [wd_ref.at[e] for e in range(own)]
    count = len(mats)

    def weight(j, k):
        wide = pl.ds(pl.multiple_of(j * UNIT, UNIT), UNIT)
        return pltpu.make_async_copy(mats[k].at[:, wide], wbuf.at[k % 2], w_sem.at[k % 2])

    def bound(way, hop):
        return (pos - 1 - hop + 2 * CHIPS) % CHIPS if way == 0 else (pos + 1 + hop) % CHIPS

    def ring(j, way, hop):
        return pltpu.make_async_remote_copy(
            src_ref=rbuf.at[way, j, hop], dst_ref=rbuf.at[way, j, hop + 1],
            send_sem=send_sem.at[way, j, hop], recv_sem=recv_sem.at[way, j, hop],
            device_id=ahead[way], device_id_type=MESH)

    def arrival(j, way, hop):
        return pltpu.make_async_remote_copy(
            src_ref=rbuf.at[way, j, hop - 1], dst_ref=rbuf.at[way, j, hop],
            send_sem=send_sem.at[way, j, hop - 1], recv_sem=recv_sem.at[way, j, hop - 1],
            device_id=ahead[way], device_id_type=MESH)

    def pair(j):
        b = j % 2
        return pltpu.make_async_remote_copy(
            src_ref=psend.at[b], dst_ref=precv.at[b], send_sem=psend_sem.at[b],
            recv_sem=precv_sem.at[b], device_id=partner, device_id_type=MESH)

    def send(j, hop):
        for way in range(2):
            half = pl.ds(way * HALF, HALF)
            mine = part[j % 3, bound(way, hop), :, half]
            if hop > 0:
                arrival(j, way, hop).wait_recv()
                mine += rbuf[way, j, hop].astype(F32)
            if hop < CHIPS - 1:
                rbuf[way, j, hop] = mine.astype(BF16)
                ring(j, way, hop).start()
            else:
                at = pl.ds(pl.multiple_of(j * UNIT + way * HALF, HALF), HALF)
                y_ref[:, at] = mine.astype(BF16)

    def product(j, k):
        weight(j, k).wait()
        if k + 1 < count:
            weight(j, k + 1).start()
        else:
            @pl.when(j + 1 < units)
            def _():
                weight(j + 1, 0).start()
        for n in range(UNIT // TILE):
            at = pl.ds(n * TILE, TILE)
            if k == 0:
                shared[:, at] = dot(hs_ref[...], wbuf[k % 2, :, at])
            else:
                e = k - 1
                r = dot(h_ref[e], wbuf[k % 2, :, at]).astype(BF16)
                for s in range(sources):
                    outs[s, pl.ds(e * pad, pad), at] = r[s * pad:(s + 1) * pad]

    def combine(j):
        for place in range(CHIPS):
            s = core * CHIPS + place
            part[j % 3, place] = dot(give_ref[s], outs[s])
            o = (1 - core) * CHIPS + place
            psend[j % 2, place] = dot(give_ref[o], outs[o]).astype(BF16)
        pair(j).start()
        part[j % 3, pos] += shared[...]

    weight(0, 0).start()

    @pl.loop(0, units + 3)
    def _(u):
        for i in range(7):
            if i == 0:
                @pl.when(jnp.logical_and(u - 3 >= 0, u - 3 < units))
                def _():
                    send(u - 3, CHIPS - 1)

                @pl.when(jnp.logical_and(u - 1 >= 0, u - 1 < units))
                def _():
                    pair(u - 1).wait()
                    for place in range(CHIPS):
                        part[(u - 1) % 3, place] += precv[(u - 1) % 2, place].astype(F32)
            back, hop = (1, i // 2) if i % 2 == 0 else (2, i // 2 + 4)

            @pl.when(jnp.logical_and(u - back >= 0, u - back < units))
            def _():
                send(u - back, hop)

            @pl.when(u < units)
            def _():
                if 1 <= i <= count:
                    product(u, i - 1)
                if i == 6:
                    combine(u)

    @pl.loop(0, units)
    def _(j):
        for way in range(2):
            for hop in range(CHIPS - 1):
                ring(j, way, hop).wait_send()


def solution(mesh):
    def step(x, expert, slot, gate, w_gate, w_up, w_down, s_gate, s_up, s_down):
        members = mesh.shape["ep"]
        experts, (tokens, top) = w_gate.shape[0], expert.shape[2:]
        d, ff = w_gate.shape[1:]
        slots = 5 * tokens * top // (4 * experts)
        own = experts // members
        pad = -(-slots // 8) * 8
        rows, total, units = own * pad, members * pad, d // UNIT
        order = [2 * chip_at(pos) + core for core in range(2) for pos in range(CHIPS)]
        dma, anywhere, vmem = pltpu.SemaphoreType.DMA, pl.BlockSpec(memory_space=pl.ANY), pl.BlockSpec(memory_space=pltpu.VMEM)

        def device(x, expert, slot, gate, w_gate, w_up, w_down, s_gate, s_up, s_down):
            x, expert, slot, gate = x[0, 0], expert[0, 0], slot[0, 0], gate[0, 0]
            me = lax.axis_index("ep")
            code = jnp.where(slot < slots, expert * pad + slot, -1).astype(F32)
            info = jnp.concatenate([code, gate.astype(BF16).astype(F32)], axis=1)
            info = lax.all_gather(info, "ep")
            info = jnp.stack([info[m] for m in order])
            row = info[..., :top].astype(jnp.int32) - me * own * pad
            weight = info[..., top:]
            take = jnp.zeros((members, rows, tokens), F32)
            give = jnp.zeros((members, tokens, rows), F32)
            for j in range(top):
                r = row[..., j]
                take += (r[:, None, :] == jnp.arange(rows)[None, :, None]).astype(F32)
                give += jnp.where(r[..., None] == jnp.arange(rows), weight[..., j, None], 0.0)
            take, give = take.astype(BF16), give.astype(BF16)
            _, h, hs = pl.pallas_call(
                gather_up,
                name="gather_up",
                out_shape=(
                    jax.ShapeDtypeStruct((2, CHIPS, tokens, d), BF16),
                    jax.ShapeDtypeStruct((own, total, ff), BF16),
                    jax.ShapeDtypeStruct((tokens, ff), BF16),
                ),
                in_specs=[anywhere, vmem] + [anywhere] * 4,
                out_specs=(anywhere,) * 3,
                scratch_shapes=[
                    pltpu.VMEM((2, own, total, ff), F32),
                    pltpu.VMEM((2, tokens, ff), F32),
                    pltpu.VMEM((members, tokens, UNIT), BF16),
                    pltpu.VMEM((own, total, UNIT), BF16),
                    pltpu.VMEM((2, UNIT, ff), BF16),
                    pltpu.VMEM((2, total, TILE), BF16),
                    dma((2, units, CHIPS)), dma((2, units, CHIPS)), dma((2, units, CHIPS)),
                    dma((2, units, CHIPS)), dma((members,)), dma((2,)), dma((2,)),
                ],
                compiler_params=pltpu.CompilerParams(
                    collective_id=0, has_side_effects=True, vmem_limit_bytes=67_043_328),
            )(x, take, w_gate, w_up, s_gate, s_up)
            y = pl.pallas_call(
                down_scatter,
                name="down_scatter",
                out_shape=jax.ShapeDtypeStruct((tokens, d), BF16),
                in_specs=[vmem] * 3 + [anywhere] * 2,
                out_specs=vmem,
                scratch_shapes=[
                    pltpu.VMEM((3, CHIPS, tokens, UNIT), F32),
                    pltpu.VMEM((tokens, UNIT), F32),
                    pltpu.VMEM((2, CHIPS, tokens, UNIT), BF16),
                    pltpu.VMEM((2, CHIPS, tokens, UNIT), BF16),
                    pltpu.VMEM((members, rows, UNIT), BF16),
                    pltpu.VMEM((2, ff, UNIT), BF16),
                    pltpu.VMEM((2, units, CHIPS, tokens, HALF), BF16),
                    dma((2, units, CHIPS)), dma((2, units, CHIPS)), dma((2,)), dma((2,)), dma((2,)),
                ],
                compiler_params=pltpu.CompilerParams(
                    collective_id=1, has_side_effects=True, vmem_limit_bytes=67_043_328),
            )(h, hs, give, w_down, s_down)
            return y[None, None]

        tok, exp, rep = P("dp", "ep"), P("ep"), P()
        return jax.shard_map(
            device, mesh=mesh,
            in_specs=(tok, tok, tok, tok, exp, exp, exp, rep, rep, rep),
            out_specs=tok, check_vma=False,
        )(x, expert, slot, gate, w_gate, w_up, w_down, s_gate, s_up, s_down)

    return step
```

time: 690 us -> 485 us (0.70)
  Pallas kernels: 0 us -> 436 us
  waiting for transfers between devices: 380 us -> 0 us
  matrix products: 235 us -> 0 us
  local copies, waits for them, and re-layouts: 33.4 us -> 5.86 us
  other arithmetic: 1.44 us -> 17.8 us
  between operations: 13.8 us -> 0.26 us
    pallas_call x0 -> x2, Pallas kernels: none -> 436 us  [the longest x1 246 us: device(): pl.pallas_call(gather_up, name='gather_up', out_shape=(jax.ShapeDtypeStru...]
    reduce_scatter x1 -> x0, waiting for transfers between devices: 253 us -> none  [device(): y = lax.psum_scatter(part, 'ep', scatter_dimension=0)]
    dot_general x8 -> x0, matrix products: 235 us -> none  [mm(): return jnp.einsum(form, a, b, preferred_element_type=jnp.float32)]
    all_gather x1 -> x0, waiting for transfers between devices: 126 us -> none  [device(): xs = lax.all_gather(x, 'ep')]
    transpose x2 -> x0, local copies, waits for them, and re-layouts: 31.1 us -> none  [the longest x1 15.6 us: device(): z.reshape(members, own, pad, -1).transpose(1, 0, 2, 3)]
    convert_element_type x2 -> x4, other arithmetic: 1.42 us -> 17.7 us  [the longest x2 16.3 us: device(): take, give = (take.astype(BF16), give.astype(BF16))]
  transfers between devices with their start and end apart: 2 -> 0, of which waited for: 2 -> 0; matrix products, arithmetic and copies ran while one was open for 3% -> 0% of each run, Pallas kernels for 0% -> 0%
where the time goes in v2:
time: 485 us; the launch traced here: 484 us
  Pallas kernels  436 us (90%)
  blocking collectives  24.2 us (5%)
  other arithmetic  17.8 us (4%)
  local copies, waits for them, and re-layouts  5.86 us (1%)
    pallas_call x1, Pallas kernels, device(): pl.pallas_call(gather_up, name='gather_up', out_shape=(jax.ShapeDtypeStru...  246 us
    pallas_call x1, Pallas kernels, device(): pl.pallas_call(down_scatter, name='down_scatter', out_shape=jax.ShapeDtyp...  190 us
    all_gather x1, blocking collectives, device(): info = lax.all_gather(info, 'ep')  24.2 us
    convert_element_type x2, other arithmetic, device(): take, give = (take.astype(BF16), give.astype(BF16))  16.3 us

profile of v2, /device:TPU:0, one launch (start us, length us, event | category | flops | bytes accessed | tf_op | source)
XLA Modules:
  0.0 484.0 jit_solution(1335643197561234468)
XLA Ops:
  0.0 0.7 bitcast_convert_fusion
  0.7 0.7 convert_bitcast_fusion
  1.4 24.2 %all-gather = f32[4096,16]{0,1:T(8,128)S(1)} all-gather(f32[256,16]{0,1:T(8,128)S(1)} %pad_maximum_fusion), channel_id=2, replica_groups=mesh['dp'=2,'ep'=16] {'ep'}, dimensions={0}, use_global_device_ids=true | all-gather | bytes 278528 | tf_op jit(solution)/shard_map/all_gather | solution.py:363
  25.8 0.0 copy-start
  25.8 0.1 fusion.2
  25.9 0.6 copy-done
  26.5 0.0 copy-start.1
  26.5 0.0 copy-start.2
  26.5 0.0 copy-start.3
  26.5 0.0 copy-start.4
  26.5 0.0 copy-start.5
  26.5 0.0 copy-start.6
  26.6 0.0 copy-start.7
  26.6 0.0 copy-start.8
  26.6 0.5 copy-done.1
  27.1 0.0 copy-done.2
  27.1 0.0 copy-done.3
  27.1 0.0 copy-done.4
  27.1 0.0 copy-done.5
  27.1 0.0 copy-done.6
  27.1 0.0 copy-done.7
  27.2 0.0 copy-done.8
  27.2 4.1 add_convert_fusion.1.take_ref
  31.3 246.1 %gather_up.1 = (bf16[2,8,256,3584]{3,2,1,0:T(8,128)(2,1)}, bf16[3,896,2048]{2,1,0:T(8,128)(2,1)}, bf16[256,2048]{1,0:T(8,128)(2,1)}) custom-call(bf16[256,3584]{1,0:T(8,128)(2,1)} %bitcast.104, bf16[16,168,256]{2,1,0:T(8,128)(2,1)} %add_convert_fusion.1.take_ref, bf16[3,3584,2048]{2,1,0:T(8,128)(2,1)} %wg_ref.1, bf16[3,3584,2048]{2,1,0:T(8,128)(2,1)} %wu_ref.1, ...), custom_call_target="tpu_custom_call" | custom-call | tf_op jit(solution)/shard_map/gather_up/pallas_call | solution.py:374
  277.4 1.7 fusion.1
  279.1 12.3 %add_convert_fusion.give_ref = bf16[16,256,168]{2,1,0:T(8,128)(2,1)} fusion(f32[16,256]{1,0:T(8,128)S(1)} %get-tuple-element.33, s32[16,256]{1,0:T(8,128)} %copy-done.1, f32[16,256]{1,0:T(8,128)S(1)} %get-tuple-element.34, s32[16,256]{1,0:T(8,128)} %copy-done.2, f32[16,256]{1,0:T(8,128)S(1)} %get-tuple-element.35, s32[16,256]{1,0:T(8,128)} %copy-done.3, ...), kind=kLoop, calls=%fused_computation | loop fusion | flops 16515072 | bytes 1638400 | tf_op jit(solution)/shard_map/convert_element_type | solution.py:373
  291.4 189.8 %down_scatter.1 = bf16[256,3584]{1,0:T(8,128)(2,1)} custom-call(bf16[3,896,2048]{2,1,0:T(8,128)(2,1)} %get-tuple-element.7.h_ref, bf16[256,2048]{1,0:T(8,128)(2,1)} %get-tuple-element.8.hs_ref, bf16[16,256,168]{2,1,0:T(8,128)(2,1)} %add_convert_fusion.give_ref, bf16[3,2048,3584]{2,1,0:T(8,128)(2,1)} %wd_ref.1, bf16[2048,3584]{1,0:T(8,128)(2,1)} %sd_ref.1), custom_call_target="tpu_custom_call" | custom-call | tf_op jit(solution)/shard_map/down_scatter/pallas_call | solution.py:397
  481.2 2.8 copy.59
  (26 shorter events, 0.1 us)
Async XLA Ops:
  25.8 0.7 copy-start
  26.5 0.6 copy-start.1
  26.5 0.6 copy-start.2
  26.5 0.6 copy-start.3
  26.5 0.6 copy-start.4
  26.5 0.6 copy-start.5
  26.5 0.6 copy-start.6
  26.6 0.6 copy-start.7
  26.6 0.6 copy-start.8

commit v3 on v2

v3 whole, which is shorter than its diff:
```python
import functools

import jax
import jax.numpy as jnp
from jax import lax
from jax.experimental import pallas as pl
from jax.experimental.pallas import tpu as pltpu
from jax.sharding import PartitionSpec as P

MESH = pl.DeviceIdType.MESH
F32, BF16 = jnp.float32, jnp.bfloat16
CHIPS = 8
HALF = 256
UNIT = 2 * HALF
TILE = 256
STRIP = 256
DEPTH = 5


def dot(a, b):
    return jnp.dot(a, b, preferred_element_type=F32)


def tdot(a, b):
    return lax.dot_general(a, b, (((0,), (0,)), ((), ())), preferred_element_type=F32)


def chip_at(pos):
    return pos + pos // 4 * (11 - 2 * pos)


def places():
    me = lax.axis_index("ep")
    core, pos = me % 2, chip_at(me // 2)

    def device(pos, core):
        return (lax.axis_index("dp"), 2 * chip_at(pos) + core)

    right, left = device((pos + 1) % CHIPS, core), device((pos + CHIPS - 1) % CHIPS, core)
    return core, pos, right, left, device(pos, 1 - core)


def meet(devices):
    barrier = pltpu.get_barrier_semaphore()
    for d in devices:
        pl.semaphore_signal(barrier, inc=1, device_id=d, device_id_type=MESH)
    pl.semaphore_wait(barrier, len(devices))


def gather_up(
    x_ref, info_ref, wg_ref, wu_ref, sg_ref, su_ref, all_ref, h_ref, hs_ref, give_ref,
    acc, acc_s, xbuf, z, wbuf, hbuf, info, take, give,
    send_sem, recv_sem, psend_sem, precv_sem, info_sem, load_sem, w_sem, h_sem, give_sem,
):
    own, total, ff = acc.shape[1:]
    tokens, d = x_ref.shape
    top = info_ref.shape[0] // 2
    units = d // UNIT
    sources = 2 * CHIPS
    pad = total // sources
    core, pos, right, left, partner = places()
    ahead = (right, left)
    meet((right, left, partner))

    def origin(way, hop):
        return (pos - hop + CHIPS) % CHIPS if way == 0 else (pos + hop) % CHIPS

    def block(j, way, hop, color):
        at = pl.ds(pl.multiple_of(j * UNIT + way * HALF, HALF), HALF)
        return all_ref.at[color, origin(way, hop), :, at]

    def mine(j, way):
        return x_ref.at[:, pl.ds(pl.multiple_of(j * UNIT + way * HALF, HALF), HALF)]

    def ring(j, way, hop, src=None):
        here = block(j, way, hop, core)
        return pltpu.make_async_remote_copy(
            src_ref=here if src is None else src, dst_ref=here, send_sem=send_sem.at[way, j, hop],
            recv_sem=recv_sem.at[way, j, hop], device_id=ahead[way], device_id_type=MESH)

    def arrival(j, way, hop):
        there = block(j, way, hop, core)
        return pltpu.make_async_remote_copy(
            src_ref=there, dst_ref=there, send_sem=send_sem.at[way, j, hop - 1],
            recv_sem=recv_sem.at[way, j, hop - 1], device_id=ahead[way], device_id_type=MESH)

    def pair(j, way, hop, src=None):
        here = block(j, way, hop, core)
        return pltpu.make_async_remote_copy(
            src_ref=here if src is None else src, dst_ref=here, send_sem=psend_sem.at[way, j, hop],
            recv_sem=precv_sem.at[way, j, hop], device_id=partner, device_id_type=MESH)

    def pair_arrival(j, way, hop):
        there = block(j, way, hop, 1 - core)
        return pltpu.make_async_remote_copy(
            src_ref=there, dst_ref=there, send_sem=psend_sem.at[way, j, hop],
            recv_sem=precv_sem.at[way, j, hop], device_id=partner, device_id_type=MESH)

    def note(hop, to_pair, src=None):
        here = info.at[core, origin(0, hop)]
        return pltpu.make_async_remote_copy(
            src_ref=here if src is None else src, dst_ref=here, send_sem=info_sem.at[to_pair, 0, hop],
            recv_sem=info_sem.at[to_pair, 1, hop], device_id=partner if to_pair else right, device_id_type=MESH)

    def note_arrival(hop, to_pair):
        there = info.at[1 - core if to_pair else core, origin(0, hop)]
        n = hop if to_pair else hop - 1
        return pltpu.make_async_remote_copy(
            src_ref=there, dst_ref=there, send_sem=info_sem.at[to_pair, 0, n],
            recv_sem=info_sem.at[to_pair, 1, n], device_id=partner if to_pair else right, device_id_type=MESH)

    def load(j, color, place):
        wide = pl.ds(pl.multiple_of(j * UNIT, UNIT), UNIT)
        s = color * CHIPS + place
        return pltpu.make_async_copy(all_ref.at[color, place, :, wide], xbuf.at[s], load_sem.at[s])

    def load_own(j):
        wide = pl.ds(pl.multiple_of(j * UNIT, UNIT), UNIT)
        s = core * CHIPS + pos
        return pltpu.make_async_copy(x_ref.at[:, wide], xbuf.at[s], load_sem.at[s])

    last = 2 * own + 1

    def weight(j, k, mat):
        rows = pl.ds(pl.multiple_of(j * UNIT, UNIT), UNIT)
        return pltpu.make_async_copy(mat.at[rows, :], wbuf.at[k % 2], w_sem.at[k % 2])

    def send(j, hop):
        @pl.when(hop == 0)
        def _():
            @pl.when(j == 0)
            def _():
                note(0, 0, info_ref).start()
                note(0, 1, info_ref).start()
            for way in range(2):
                ring(j, way, 0, mine(j, way)).start()
                pair(j, way, 0, mine(j, way)).start()

        @pl.when(hop > 0)
        def _():
            @pl.when(j == 0)
            def _():
                note_arrival(hop, 0).wait_recv()
                note(hop, 0).start()
                note(hop, 1).start()
            for way in range(2):
                arrival(j, way, hop).wait_recv()
                ring(j, way, hop).start()
                pair(j, way, hop).start()

    def accumulate(lhs, w, total_ref):
        for n in range(0, ff, UNIT):
            at = pl.ds(n, UNIT)
            total_ref[:, at] += dot(lhs[...], w[:, at])

    def product(j, k):
        weight(j, k, wg_ref.at[0]).wait()
        e = (k - 1) // 2

        @pl.when(jnp.logical_and(k < last, k % 2 == 1))
        def _():
            weight(j, k + 1, wg_ref.at[e]).start()

        @pl.when(jnp.logical_and(k < last, k % 2 == 0))
        def _():
            weight(j, k + 1, wu_ref.at[e]).start()

        @pl.when(jnp.logical_and(k == last, j + 1 < units))
        def _():
            weight(j + 1, 0, sg_ref).start()
        accumulate(z.at[(k - 2) // 2], wbuf.at[k % 2], acc.at[k % 2, (k - 2) // 2])

    def shared(j):
        weight(j, 0, sg_ref).wait()
        weight(j, 1, su_ref).start()
        accumulate(xbuf.at[core * CHIPS + pos], wbuf.at[0], acc_s.at[0])
        weight(j, 1, su_ref).wait()
        weight(j, 2, wg_ref.at[0]).start()
        accumulate(xbuf.at[core * CHIPS + pos], wbuf.at[1], acc_s.at[1])

    def route():
        note_arrival(CHIPS - 1, 0).wait_recv()
        note(CHIPS - 1, 1).start()
        for hop in range(CHIPS):
            note_arrival(hop, 1).wait_recv()
        info[core, pos] = info_ref[...]
        base = (lax.axis_index("ep") * own * pad).astype(F32)

        @pl.loop(0, sources)
        def _(s):
            here = info[s // CHIPS, s % CHIPS]
            row = lax.broadcasted_iota(jnp.int32, (own * pad, tokens), 0).astype(F32)
            picked = jnp.zeros((own * pad, tokens), F32)
            gates = jnp.zeros((own * pad, tokens), F32)
            for n in range(top):
                hit = row == here[n:n + 1] - base
                picked = jnp.where(hit, 1.0, picked)
                gates = jnp.where(hit, here[top + n:top + n + 1], gates)
            take[s] = picked.astype(BF16)
            give[s] = gates.astype(BF16)
        pltpu.make_async_copy(give, give_ref, give_sem.at[0]).start()

    def dispatch(j):
        for way in range(2):
            pair_arrival(j, way, CHIPS - 1).wait_recv()
        for hop in (1, CHIPS - 1):
            load(j, 1 - core, origin(0, hop)).start()
        load_own(j).wait()
        for hop in range(1, CHIPS):
            load(j, core, origin(0, hop)).wait()
        for hop in range(CHIPS):
            load(j, 1 - core, origin(0, hop)).wait()
        for s in range(sources):
            rows = dot(take[s], xbuf[s]).astype(BF16)
            for e in range(own):
                z[e, pl.ds(s * pad, pad), :] = rows[e * pad:(e + 1) * pad]

    def fetch(j):
        for way in range(2):
            arrival(j, way, CHIPS - 1).wait_recv()
            pair(j, way, CHIPS - 1).start()
        load_own(j).start()
        for hop in range(1, CHIPS):
            load(j, core, origin(0, hop)).start()
        for hop in range(CHIPS - 1):
            for way in range(2):
                pair_arrival(j, way, hop).wait_recv()
        for hop in (0, *range(2, CHIPS - 1)):
            load(j, 1 - core, origin(0, hop)).start()

    def finish(e):
        gate = acc_s.at[0] if e == own else acc.at[0, e]
        up = acc_s.at[1] if e == own else acc.at[1, e]
        n_rows = tokens if e == own else total
        out = hs_ref if e == own else h_ref.at[e]

        def put(n, b):
            at = pl.ds(pl.multiple_of(n * TILE, TILE), TILE)
            return pltpu.make_async_copy(hbuf.at[b, pl.ds(0, n_rows)], out.at[:, at], h_sem.at[b])

        @pl.loop(0, ff // TILE, step=2)
        def _(n):
            for b in range(2):
                at = pl.ds(pl.multiple_of((n + b) * TILE, TILE), TILE)

                @pl.when(n > 0)
                def _():
                    put(n + b - 2, b).wait()
                g = 0.5 * gate[:, at]
                hbuf[b, pl.ds(0, n_rows)] = ((g + g * jnp.tanh(g)) * up[:, at]).astype(BF16)
                put(n + b, b).start()
        for b in range(2):
            put(ff // TILE - 2 + b, b).wait()

    weight(0, 0, sg_ref).start()

    def clear():
        @pl.loop(0, ff // TILE)
        def _(n):
            at = pl.ds(pl.multiple_of(n * TILE, TILE), TILE)
            for g in range(2):
                acc_s[g, :, at] = jnp.zeros((tokens, TILE), F32)
                for e in range(own):
                    acc[g, e, :, at] = jnp.zeros((total, TILE), F32)

    def real(j):
        return jnp.logical_and(j >= 0, j < units)

    @pl.loop(0, 7 * (units + 4))
    def _(t):
        u, i = t // 7, t % 7
        hop = 5 * i % 7
        back = (3 * hop - i) // 7

        @pl.when(real(u - back))
        def _():
            send(u - back, hop)

        @pl.when(t == 1)
        def _():
            clear()
        now = u - 3

        @pl.when(jnp.logical_and(i == 0, real(now)))
        def _():
            fetch(now)

        @pl.when(jnp.logical_and(i == 1, real(now)))
        def _():
            @pl.when(now == 0)
            def _():
                route()
            dispatch(now)
            shared(now)
        wrap = (6 - i) // 6

        @pl.when(jnp.logical_and(i != 1, real(now - wrap)))
        def _():
            product(now - wrap, i + 7 * wrap)

    for e in (own, *range(own)):
        finish(e)
    pltpu.make_async_copy(give, give_ref, give_sem.at[0]).wait()

    @pl.loop(0, units)
    def _(j):
        for way in range(2):
            for hop in range(CHIPS - 1):
                ring(j, way, hop).wait_send()
            for hop in range(CHIPS):
                pair(j, way, hop).wait_send()
    for hop in range(CHIPS):
        if hop < CHIPS - 1:
            note(hop, 0).wait_send()
        note(hop, 1).wait_send()


def down_scatter(
    h_ref, hs_ref, give_ref, wd_ref, sd_ref, y_ref,
    part, shared, psend, precv, outs, wbuf, rbuf,
    send_sem, recv_sem, psend_sem, precv_sem, w_sem,
):
    own, total, ff = h_ref.shape
    tokens, d = y_ref.shape
    units = d // STRIP
    sources = 2 * CHIPS
    pad = total // sources
    core, pos, right, left, partner = places()
    ahead = (right, left)
    meet((right, left, partner))

    mats = [sd_ref] + [wd_ref.at[e] for e in range(own)]
    count = len(mats)

    def weight(j, k):
        wide = pl.ds(pl.multiple_of(j * STRIP, STRIP), STRIP)
        return pltpu.make_async_copy(mats[k].at[:, wide], wbuf.at[k % 2], w_sem.at[k % 2])

    def bound(way, hop):
        return (pos - 1 - hop + 2 * CHIPS) % CHIPS if way == 0 else (pos + 1 + hop) % CHIPS

    def ring(j, way, hop):
        return pltpu.make_async_remote_copy(
            src_ref=rbuf.at[way, j, hop], dst_ref=rbuf.at[way, j, hop + 1],
            send_sem=send_sem.at[way, j, hop], recv_sem=recv_sem.at[way, j, hop],
            device_id=ahead[way], device_id_type=MESH)

    def arrival(j, way, hop):
        return pltpu.make_async_remote_copy(
            src_ref=rbuf.at[way, j, hop - 1], dst_ref=rbuf.at[way, j, hop],
            send_sem=send_sem.at[way, j, hop - 1], recv_sem=recv_sem.at[way, j, hop - 1],
            device_id=ahead[way], device_id_type=MESH)

    def pair(j):
        b = j % 2
        return pltpu.make_async_remote_copy(
            src_ref=psend.at[b], dst_ref=precv.at[b], send_sem=psend_sem.at[b],
            recv_sem=precv_sem.at[b], device_id=partner, device_id_type=MESH)

    def send(j, hop):
        for way in range(2):
            half = pl.ds(way * STRIP // 2, STRIP // 2)
            mine = part[j % DEPTH, bound(way, hop), :, half]
            if hop > 0:
                arrival(j, way, hop).wait_recv()
                mine += rbuf[way, j, hop].astype(F32)
            if hop < CHIPS - 1:
                rbuf[way, j, hop] = mine.astype(BF16)
                ring(j, way, hop).start()
            else:
                at = pl.ds(pl.multiple_of(j * STRIP + way * STRIP // 2, STRIP // 2), STRIP // 2)
                y_ref[:, at] = mine.astype(BF16)

    def product(j, k):
        weight(j, k).wait()
        if k + 1 < count:
            weight(j, k + 1).start()
        else:
            @pl.when(j + 1 < units)
            def _():
                weight(j + 1, 0).start()
        if k == 0:
            shared[...] = dot(hs_ref[...], wbuf[k % 2])
        else:
            e = k - 1
            r = dot(h_ref[e], wbuf[k % 2]).astype(BF16)
            for s in range(sources):
                outs[s, pl.ds(e * pad, pad), :] = r[s * pad:(s + 1) * pad]

    def combine(j):
        for place in range(CHIPS):
            s = core * CHIPS + place
            part[j % DEPTH, place] = tdot(give_ref[s], outs[s])
            o = (1 - core) * CHIPS + place
            psend[j % 2, place] = tdot(give_ref[o], outs[o]).astype(BF16)
        pair(j).start()
        part[j % DEPTH, pos] += shared[...]

    weight(0, 0).start()

    def when_real(j, act, *args):
        @pl.when(jnp.logical_and(j >= 0, j < units))
        def _():
            act(j, *args)

    def pair_sum(j):
        pair(j).wait()
        for place in range(CHIPS):
            part[j % DEPTH, place] += precv[j % 2, place].astype(F32)

    @pl.loop(0, units + DEPTH)
    def _(u):
        when_real(u - DEPTH, send, CHIPS - 1)
        when_real(u - 1, pair_sum)
        for i in range(7):
            hop = 2 * i % 7
            when_real(u - 1 - (4 * hop - i) // 7, send, hop)
            if 1 <= i <= count:
                when_real(u, product, i - 1)
            if i == 6:
                when_real(u, combine)

    @pl.loop(0, units)
    def _(j):
        for way in range(2):
            for hop in range(CHIPS - 1):
                ring(j, way, hop).wait_send()


def solution(mesh):
    def step(x, expert, slot, gate, w_gate, w_up, w_down, s_gate, s_up, s_down):
        members = mesh.shape["ep"]
        experts, (tokens, top) = w_gate.shape[0], expert.shape[2:]
        d, ff = w_gate.shape[1:]
        slots = 5 * tokens * top // (4 * experts)
        own = experts // members
        pad = -(-slots // 8) * 8
        rows, total = own * pad, members * pad
        units, strips = d // UNIT, d // STRIP
        dma, anywhere, vmem = pltpu.SemaphoreType.DMA, pl.BlockSpec(memory_space=pl.ANY), pl.BlockSpec(memory_space=pltpu.VMEM)

        def device(x, expert, slot, gate, w_gate, w_up, w_down, s_gate, s_up, s_down):
            x, expert, slot, gate = x[0, 0], expert[0, 0], slot[0, 0], gate[0, 0]
            code = jnp.where(slot < slots, expert * pad + slot, -1).astype(F32)
            info = jnp.concatenate([code.T, gate.astype(BF16).astype(F32).T])
            _, h, hs, give = pl.pallas_call(
                gather_up,
                name="gather_up",
                out_shape=(
                    jax.ShapeDtypeStruct((2, CHIPS, tokens, d), BF16),
                    jax.ShapeDtypeStruct((own, total, ff), BF16),
                    jax.ShapeDtypeStruct((tokens, ff), BF16),
                    jax.ShapeDtypeStruct((members, rows, tokens), BF16),
                ),
                in_specs=[anywhere, vmem] + [anywhere] * 4,
                out_specs=(anywhere,) * 4,
                scratch_shapes=[
                    pltpu.VMEM((2, own, total, ff), F32),
                    pltpu.VMEM((2, tokens, ff), F32),
                    pltpu.VMEM((members, tokens, UNIT), BF16),
                    pltpu.VMEM((own, total, UNIT), BF16),
                    pltpu.VMEM((2, UNIT, ff), BF16),
                    pltpu.VMEM((2, total, TILE), BF16),
                    pltpu.VMEM((2, CHIPS, 2 * top, tokens), F32),
                    pltpu.VMEM((members, rows, tokens), BF16),
                    pltpu.VMEM((members, rows, tokens), BF16),
                    dma((2, units, CHIPS)), dma((2, units, CHIPS)), dma((2, units, CHIPS)),
                    dma((2, units, CHIPS)), dma((2, 2, CHIPS)), dma((members,)), dma((2,)), dma((2,)), dma((1,)),
                ],
                compiler_params=pltpu.CompilerParams(
                    collective_id=0, has_side_effects=True, vmem_limit_bytes=67_043_328),
            )(x, info, w_gate, w_up, s_gate, s_up)
            y = pl.pallas_call(
                down_scatter,
                name="down_scatter",
                out_shape=jax.ShapeDtypeStruct((tokens, d), BF16),
                in_specs=[vmem] * 3 + [anywhere] * 2,
                out_specs=vmem,
                scratch_shapes=[
                    pltpu.VMEM((DEPTH, CHIPS, tokens, STRIP), F32),
                    pltpu.VMEM((tokens, STRIP), F32),
                    pltpu.VMEM((2, CHIPS, tokens, STRIP), BF16),
                    pltpu.VMEM((2, CHIPS, tokens, STRIP), BF16),
                    pltpu.VMEM((members, rows, STRIP), BF16),
                    pltpu.VMEM((2, ff, STRIP), BF16),
                    pltpu.VMEM((2, strips, CHIPS, tokens, STRIP // 2), BF16),
                    dma((2, strips, CHIPS)), dma((2, strips, CHIPS)), dma((2,)), dma((2,)), dma((2,)),
                ],
                compiler_params=pltpu.CompilerParams(
                    collective_id=1, has_side_effects=True, vmem_limit_bytes=67_043_328),
            )(h, hs, give, w_down, s_down)
            return y[None, None]

        tok, exp, rep = P("dp", "ep"), P("ep"), P()
        return jax.shard_map(
            device, mesh=mesh,
            in_specs=(tok, tok, tok, tok, exp, exp, exp, rep, rep, rep),
            out_specs=tok, check_vma=False,
        )(x, expert, slot, gate, w_gate, w_up, w_down, s_gate, s_up, s_down)

    return step
```

time: 485 us -> 394 us (0.81)
  Pallas kernels: 436 us -> 386 us
  blocking collectives: 24.2 us -> 0 us
  other arithmetic: 17.8 us -> 2.02 us
    pallas_call x1, Pallas kernels: 246 us -> 209 us  [device(): pl.pallas_call(gather_up, name='gather_up', out_shape=(jax.ShapeDtypeStru...]
    all_gather x1 -> x0, blocking collectives: 24.2 us -> none  [device(): info = lax.all_gather(info, 'ep')]
    convert_element_type x4 -> x0, other arithmetic: 17.7 us -> none  [the longest x2 16.3 us: device(): take, give = (take.astype(BF16), give.astype(BF16))]
    pallas_call x1, Pallas kernels: 190 us -> 178 us  [device(): pl.pallas_call(down_scatter, name='down_scatter', out_shape=jax.ShapeDtyp...]
where the time goes in v3:
time: 394 us; the launch traced here: 391 us
  Pallas kernels  386 us (98%)
    pallas_call x1, Pallas kernels, device(): pl.pallas_call(gather_up, name='gather_up', out_shape=(jax.ShapeDtypeStru...  209 us
    pallas_call x1, Pallas kernels, device(): pl.pallas_call(down_scatter, name='down_scatter', out_shape=jax.ShapeDtyp...  178 us

profile of v3, /device:TPU:0, one launch (start us, length us, event | category | flops | bytes accessed | tf_op | source)
XLA Modules:
  0.0 391.2 jit_solution(3858425323384849605)
XLA Ops:
  0.0 0.7 convert_bitcast_fusion.1
  0.7 0.7 convert_bitcast_fusion
  1.4 0.6 pad_maximum_fusion.info_ref
  2.0 208.7 %gather_up.1 = (bf16[2,8,256,3584]{3,2,1,0:T(8,128)(2,1)}, bf16[3,896,2048]{2,1,0:T(8,128)(2,1)}, bf16[256,2048]{1,0:T(8,128)(2,1)}, bf16[16,168,256]{2,1,0:T(8,128)(2,1)}) custom-call(bf16[256,3584]{1,0:T(8,128)(2,1)} %bitcast.12, f32[16,256]{1,0:T(8,128)} %pad_maximum_fusion.info_ref, bf16[3,3584,2048]{2,1,0:T(8,128)(2,1)} %wg_ref.1, ...), custom_call_target="tpu_custom_call" | custom-call | tf_op jit(solution)/shard_map/gather_up/pallas_call | solution.py:446
  210.8 177.6 %down_scatter.1 = bf16[256,3584]{1,0:T(8,128)(2,1)} custom-call(bf16[3,896,2048]{2,1,0:T(8,128)(2,1)} %get-tuple-element.8.h_ref, bf16[256,2048]{1,0:T(8,128)(2,1)} %get-tuple-element.9.hs_ref, bf16[16,168,256]{2,1,0:T(8,128)(2,1)} %get-tuple-element.10.give_ref, bf16[3,2048,3584]{2,1,0:T(8,128)(2,1)} %wd_ref.1, bf16[2048,3584]{1,0:T(8,128)(2,1)} %sd_ref.1), custom_call_target="tpu_custom_call" | custom-call | tf_op jit(solution)/shard_map/down_scatter/pallas_call | solution.py:473
  388.4 2.8 copy.12

commit v4 on v3

--- a/solution.py
+++ b/solution.py
@@ -14,7 +14,8 @@
 UNIT = 2 * HALF
 TILE = 256
 STRIP = 256
-DEPTH = 5
+GATHER, SCATTER = 3, 5
+DEPTH = SCATTER + 1
 
 
 def dot(a, b):
@@ -168,7 +169,34 @@
         @pl.when(jnp.logical_and(k == last, j + 1 < units))
         def _():
             weight(j + 1, 0, sg_ref).start()
-        accumulate(z.at[(k - 2) // 2], wbuf.at[k % 2], acc.at[k % 2, (k - 2) // 2])
+        e = (k - 2) // 2
+        closing = jnp.logical_and(j == units - 1, k % 2 == 1)
+
+        @pl.when(jnp.logical_not(closing))
+        def _():
+            accumulate(z.at[e], wbuf.at[k % 2], acc.at[k % 2, e])
+
+        @pl.when(closing)
+        def _():
+            close(e)
+
+    def put(e, n):
+        at = pl.ds(n * UNIT, UNIT)
+        return pltpu.make_async_copy(hbuf.at[n % 2], h_ref.at[e, :, at], h_sem.at[n % 2])
+
+    def close(e):
+        for n in range(ff // UNIT):
+            at = pl.ds(n * UNIT, UNIT)
+            if n < 2:
+                @pl.when(e > 0)
+                def _():
+                    put(e - 1, ff // UNIT - 2 + n).wait()
+            else:
+                put(e, n - 2).wait()
+            up = acc[1, e, :, at] + dot(z[e], wbuf[1, :, at])
+            g = 0.5 * acc[0, e, :, at]
+            hbuf[n % 2] = ((g + g * jnp.tanh(g)) * up).astype(BF16)
+            put(e, n).start()
 
     def shared(j):
         weight(j, 0, sg_ref).wait()
@@ -200,11 +228,13 @@
             give[s] = gates.astype(BF16)
         pltpu.make_async_copy(give, give_ref, give_sem.at[0]).start()
 
-    def dispatch(j):
+    def fetch_rest(j):
         for way in range(2):
             pair_arrival(j, way, CHIPS - 1).wait_recv()
         for hop in (1, CHIPS - 1):
             load(j, 1 - core, origin(0, hop)).start()
+
+    def dispatch(j):
         load_own(j).wait()
         for hop in range(1, CHIPS):
             load(j, core, origin(0, hop)).wait()
@@ -228,29 +258,15 @@
         for hop in (0, *range(2, CHIPS - 1)):
             load(j, 1 - core, origin(0, hop)).start()
 
-    def finish(e):
-        gate = acc_s.at[0] if e == own else acc.at[0, e]
-        up = acc_s.at[1] if e == own else acc.at[1, e]
-        n_rows = tokens if e == own else total
-        out = hs_ref if e == own else h_ref.at[e]
-
-        def put(n, b):
-            at = pl.ds(pl.multiple_of(n * TILE, TILE), TILE)
-            return pltpu.make_async_copy(hbuf.at[b, pl.ds(0, n_rows)], out.at[:, at], h_sem.at[b])
-
-        @pl.loop(0, ff // TILE, step=2)
-        def _(n):
-            for b in range(2):
-                at = pl.ds(pl.multiple_of((n + b) * TILE, TILE), TILE)
-
-                @pl.when(n > 0)
-                def _():
-                    put(n + b - 2, b).wait()
-                g = 0.5 * gate[:, at]
-                hbuf[b, pl.ds(0, n_rows)] = ((g + g * jnp.tanh(g)) * up[:, at]).astype(BF16)
-                put(n + b, b).start()
-        for b in range(2):
-            put(ff // TILE - 2 + b, b).wait()
+    def finish_shared():
+        for n in range(ff // UNIT):
+            at = pl.ds(n * UNIT, UNIT)
+            g = 0.5 * acc_s[0, :, at]
+            hbuf[n % 2, pl.ds(0, tokens)] = ((g + g * jnp.tanh(g)) * acc_s[1, :, at]).astype(BF16)
+            copy = pltpu.make_async_copy(
+                hbuf.at[n % 2, pl.ds(0, tokens)], hs_ref.at[:, at], h_sem.at[n % 2])
+            copy.start()
+            copy.wait()
 
     weight(0, 0, sg_ref).start()
 
@@ -266,11 +282,11 @@
     def real(j):
         return jnp.logical_and(j >= 0, j < units)
 
-    @pl.loop(0, 7 * (units + 4))
+    @pl.loop(0, 7 * (units + GATHER + 1))
     def _(t):
         u, i = t // 7, t % 7
-        hop = 5 * i % 7
-        back = (3 * hop - i) // 7
+        hop = pow(GATHER, -1, 7) * i % 7
+        back = (GATHER * hop - i) // 7
 
         @pl.when(real(u - back))
         def _():
@@ -279,27 +295,32 @@
         @pl.when(t == 1)
         def _():
             clear()
-        now = u - 3
+        now = u - GATHER
 
         @pl.when(jnp.logical_and(i == 0, real(now)))
         def _():
             fetch(now)
 
         @pl.when(jnp.logical_and(i == 1, real(now)))
+        def _():
+            fetch_rest(now)
+
+        @pl.when(jnp.logical_and(i == 2, real(now)))
         def _():
             @pl.when(now == 0)
             def _():
                 route()
             dispatch(now)
             shared(now)
-        wrap = (6 - i) // 6
-
-        @pl.when(jnp.logical_and(i != 1, real(now - wrap)))
-        def _():
-            product(now - wrap, i + 7 * wrap)
-
-    for e in (own, *range(own)):
-        finish(e)
+        wrap = (8 - i) // 7
+
+        @pl.when(jnp.logical_and(i != 2, real(now - wrap)))
+        def _():
+            product(now - wrap, i - 1 + 7 * wrap)
+
+    for n in (ff // UNIT - 2, ff // UNIT - 1):
+        put(own - 1, n).wait()
+    finish_shared()
     pltpu.make_async_copy(give, give_ref, give_sem.at[0]).wait()
 
     @pl.loop(0, units)
@@ -413,8 +434,8 @@
         when_real(u - DEPTH, send, CHIPS - 1)
         when_real(u - 1, pair_sum)
         for i in range(7):
-            hop = 2 * i % 7
-            when_real(u - 1 - (4 * hop - i) // 7, send, hop)
+            hop = pow(SCATTER, -1, 7) * i % 7
+            when_real(u - 1 - (SCATTER * hop - i) // 7, send, hop)
             if 1 <= i <= count:
                 when_real(u, product, i - 1)
             if i == 6:
@@ -460,7 +481,7 @@
                     pltpu.VMEM((members, tokens, UNIT), BF16),
                     pltpu.VMEM((own, total, UNIT), BF16),
                     pltpu.VMEM((2, UNIT, ff), BF16),
-                    pltpu.VMEM((2, total, TILE), BF16),
+                    pltpu.VMEM((2, total, UNIT), BF16),
                     pltpu.VMEM((2, CHIPS, 2 * top, tokens), F32),
                     pltpu.VMEM((members, rows, tokens), BF16),
                     pltpu.VMEM((members, rows, tokens), BF16),

time: 394 us -> 382 us (0.970)
  Pallas kernels: 386 us -> 375 us
    pallas_call x1, Pallas kernels: 209 us -> 200 us  [device(): pl.pallas_call(gather_up, name='gather_up', out_shape=(jax.ShapeDtypeStru...]
where the time goes in v4:
time: 382 us; the launch traced here: 380 us
  Pallas kernels  375 us (98%)
    pallas_call x1, Pallas kernels, device(): pl.pallas_call(gather_up, name='gather_up', out_shape=(jax.ShapeDtypeStru...  200 us
    pallas_call x1, Pallas kernels, device(): pl.pallas_call(down_scatter, name='down_scatter', out_shape=jax.ShapeDtyp...  176 us

profile of v4, /device:TPU:0, one launch (start us, length us, event | category | flops | bytes accessed | tf_op | source)
XLA Modules:
  0.0 380.0 jit_solution(666435350569360808)
XLA Ops:
  0.0 0.7 convert_bitcast_fusion.1
  0.7 0.7 convert_bitcast_fusion
  1.4 0.6 pad_maximum_fusion.info_ref
  2.0 199.5 %gather_up.1 = (bf16[2,8,256,3584]{3,2,1,0:T(8,128)(2,1)}, bf16[3,896,2048]{2,1,0:T(8,128)(2,1)}, bf16[256,2048]{1,0:T(8,128)(2,1)}, bf16[16,168,256]{2,1,0:T(8,128)(2,1)}) custom-call(bf16[256,3584]{1,0:T(8,128)(2,1)} %bitcast.12, f32[16,256]{1,0:T(8,128)} %pad_maximum_fusion.info_ref, bf16[3,3584,2048]{2,1,0:T(8,128)(2,1)} %wg_ref.1, ...), custom_call_target="tpu_custom_call" | custom-call | tf_op jit(solution)/shard_map/gather_up/pallas_call | solution.py:467
  201.5 175.6 %down_scatter.1 = bf16[256,3584]{1,0:T(8,128)(2,1)} custom-call(bf16[3,896,2048]{2,1,0:T(8,128)(2,1)} %get-tuple-element.8.h_ref, bf16[256,2048]{1,0:T(8,128)(2,1)} %get-tuple-element.9.hs_ref, bf16[16,168,256]{2,1,0:T(8,128)(2,1)} %get-tuple-element.10.give_ref, bf16[3,2048,3584]{2,1,0:T(8,128)(2,1)} %wd_ref.1, bf16[2048,3584]{1,0:T(8,128)(2,1)} %sd_ref.1), custom_call_target="tpu_custom_call" | custom-call | tf_op jit(solution)/shard_map/down_scatter/pallas_call | solution.py:494
  377.1 2.8 copy.12
